TPU v7x, 128 devices: a whole 4x4x4 slice. The times are simulated.
128 devices in a mesh: section: 2 (over x_hi), dp: 16 (over z, y), mp: 4 (over x_lo, core).
Axes of the slice: x: 4 (x_hi: 2, x_lo: 2; x = x_hi * 2 + x_lo), y: 4, z: 4, core: 2. Of those that a mesh axis runs over, the one named last changes fastest.
Arguments:
- text_feats: bfloat16 [16384, 512], P('dp'), may hold values from -48 to 48
- image_feats: bfloat16 [16384, 512], P(('dp', 'mp')), may hold values from -48 to 48
- logit_scale: float32 [1], replicated, may hold values from 10 to 320
- layer_inputs: bfloat16 [2, 16384, 512], P('section', 'dp'), may hold values from -6 to 6
- w_in: bfloat16 [2, 512, 2048], P('section', None, 'mp'), may hold values from -0.25 to 0.25
- w_out: bfloat16 [2, 2048, 512], P('section', 'mp'), may hold values from -0.125 to 0.125
Outputs:
- image_grad: bfloat16 [16384, 512], P(('dp', 'mp'))
- input_grad: bfloat16 [16384, 512], P('dp', 'section')
- w_in_grad: float32 [2, 512, 2048], P('section', 'dp', 'mp')
- w_out_grad_t: float32 [2, 512, 2048], P('section', 'dp', 'mp')
All inputs are finite; a program needn't handle non-finite values.
Results may differ from a plain program's by a relative error of at most 0.017.
Values may be sent and summed in bfloat16 or wider, within the bound.
No kernel may reach another device: no remote copies, remote signals or barrier semaphores. Data moves between devices by JAX's collectives and lax.ppermute only.
A program may use at most 128 MiB of HBM per device.

v0:
```python
import jax
import jax.numpy as jnp
from jax import lax
from jax.sharding import PartitionSpec as P

MICRO = 4


def from_everyone(array, axis):
    copies = jnp.broadcast_to(array, (lax.axis_size(axis), *array.shape))
    return lax.all_to_all(copies, axis, split_axis=0, concat_axis=0, tiled=True)


def collected_together(array, axis):
    leaves = jax.tree.leaves(array)
    sequence = sorted(range(len(leaves)), key=lambda k: -leaves[k].size)
    width = (1, *leaves[sequence[0]].shape)[-1]
    lines = [
        jnp.pad(leaves[k].reshape(-1), (0, -leaves[k].size % width)).reshape(-1, width)
        for k in sequence
    ]
    both, at, found = (from_everyone(jnp.concatenate(lines), axis), 0, {})
    for k, line in zip(sequence, lines):
        slab = both[:, at : at + len(line)].reshape(len(both), -1)
        found[k] = slab[:, : leaves[k].size].reshape(-1, *leaves[k].shape)
        at += len(line)
    numbers = iter(range(len(leaves)))
    return jax.tree.map(lambda _: found[next(numbers)], array)


def combined_pairwise(pieces, combine):
    while len(jax.tree.leaves(pieces)[0]) > 1:
        pieces = jax.vmap(combine)(
            *(jax.tree.map(lambda part: part[side::2], pieces) for side in (0, 1))
        )
    return jax.tree.map(lambda part: part[0], pieces)


def joined_all(array, axis, combine):
    pieces = collected_together(array, axis)
    return combined_pairwise(pieces, combine)


def of_everyone(array, axis):
    return from_everyone(array, axis).astype(jnp.float32).sum(axis=0)


def shifted(block, axis, distance):
    devices = range(lax.axis_size(axis))
    route = [(i - distance, i) for i in devices if i - distance in devices]
    return lax.ppermute(block, axis, route)


def picked(array, axis, root):
    return lax.dynamic_index_in_dim(lax.all_gather(array, axis), root, 0, keepdims=False)


def in_one_piece(arrays, axis, dim, along):
    both = jnp.concatenate(arrays, axis=along)
    result, at, done = (lax.psum_scatter(both, axis, scatter_dimension=dim, tiled=True), 0, [])
    for a in arrays:
        done.append(lax.slice_in_dim(result, at, at + a.shape[along], axis=along))
        at += a.shape[along]
    return tuple(done)


def unit_rows(values):
    wide = values.astype(jnp.float32)
    length = jnp.sqrt(jnp.sum(wide * wide, axis=1, keepdims=True) + 1.0)
    return (wide / length, length)


def unit_backward(unit, length, grad_unit):
    return (grad_unit - unit * jnp.sum(unit * grad_unit, axis=1, keepdims=True)) / length


def quick_gelu(values):
    return values * jax.nn.sigmoid(1.702 * values)


def quick_slope(values):
    sigm = jax.nn.sigmoid(1.702 * values)
    return sigm + 1.702 * values * sigm * (1.0 - sigm)


def joined_softmax(left_pair, right_pair):
    peak_value = jnp.maximum(left_pair[0], right_pair[0])
    total = left_pair[1] * jnp.exp(left_pair[0] - peak_value) + right_pair[1] * jnp.exp(
        right_pair[0] - peak_value
    )
    return (peak_value, total)


def contract_rows(left_side, right_side):
    return lax.dot_general(
        left_side, right_side, (((0,), (0,)), ((), ())), preferred_element_type=jnp.float32
    )


def contract_cols(left_side, right_side):
    return lax.dot_general(
        left_side, right_side, (((1,), (1,)), ((), ())), preferred_element_type=jnp.float32
    )


def body(text_feats, image_feats, logit_scale, layer_inputs, w_in, w_out):
    logit_mult = logit_scale[0]
    mp_count = lax.axis_size("mp")
    segment_count = lax.axis_size("section")
    dp_index = lax.axis_index("dp")
    mp_index = lax.axis_index("mp")
    segment_index = lax.axis_index("section")
    row_count = text_feats.shape[0]
    own_rows = image_feats.shape[0]
    text_unit, text_length = unit_rows(text_feats)
    image_unit, image_length = unit_rows(image_feats)
    text_low = text_unit.astype(jnp.bfloat16)
    image_low = image_unit.astype(jnp.bfloat16)
    columns = lax.all_gather(image_low, "dp", axis=0, tiled=True)
    column_total_count = columns.shape[0]
    scores = logit_mult * contract_cols(text_low, columns)
    text_ids = dp_index * row_count + jnp.arange(row_count, dtype=jnp.int32)
    column_pos = jnp.arange(column_total_count, dtype=jnp.int32)
    image_ids = (column_pos // own_rows * mp_count + mp_index) * own_rows + column_pos % own_rows
    positive = (text_ids[:, None] == image_ids[None, :]).astype(jnp.float32)
    local_rpeak = jnp.max(scores, axis=1)
    local_cpeak = jnp.max(scores, axis=0)
    row_peak, row_total = joined_all(
        (local_rpeak, jnp.sum(jnp.exp(scores - local_rpeak[:, None]), axis=1)), "mp", joined_softmax
    )
    column_local = jnp.sum(jnp.exp(scores - local_cpeak[None, :]), axis=0)
    column_peak, column_total = joined_all((local_cpeak, column_local), "dp", joined_softmax)
    row_prob = jnp.exp(scores - row_peak[:, None]) / row_total[:, None]
    column_prob = jnp.exp(scores - column_peak[None, :]) / column_total[None, :]
    score_grad = (0.5 * (row_prob + column_prob) - positive).astype(jnp.bfloat16)
    text_share = logit_mult * jnp.dot(score_grad, columns, preferred_element_type=jnp.float32)
    text_unit_grad = of_everyone(text_share.astype(jnp.bfloat16), "mp").astype(jnp.float32)
    top_grad = unit_backward(text_unit, text_length, text_unit_grad).astype(jnp.bfloat16)
    image_unit_grad = lax.psum_scatter(
        (logit_mult * contract_rows(score_grad, text_low)).astype(jnp.bfloat16),
        "dp",
        scatter_dimension=0,
        tiled=True,
    ).astype(jnp.float32)
    image_grad = unit_backward(image_unit, image_length, image_unit_grad).astype(jnp.bfloat16)
    segment_inputs = layer_inputs[0]
    w_first = w_in[0]
    w_second = w_out[0]
    step_rows = row_count // MICRO
    last_segment = segment_count - 1
    time_steps = MICRO + segment_count - 1
    is_last = segment_index == last_segment
    is_first = segment_index == 0
    incoming = jnp.zeros((step_rows, segment_inputs.shape[1]), jnp.bfloat16)
    grad_first = jnp.zeros(w_first.shape, jnp.float32)
    grad_second = jnp.zeros(w_first.shape, jnp.float32)
    finished = jnp.zeros((row_count, segment_inputs.shape[1]), jnp.bfloat16)
    for time_step in range(time_steps):
        micro_slot = time_step - last_segment + segment_index
        active = jnp.logical_and(micro_slot >= 0, micro_slot < MICRO)
        row_start = jnp.clip(micro_slot, 0, MICRO - 1) * step_rows
        top_start = min(time_step, MICRO - 1) * step_rows
        top_piece = top_grad[top_start : top_start + step_rows]
        grad_now = jnp.where(is_last, top_piece, incoming)
        inputs_now = lax.dynamic_slice_in_dim(segment_inputs, row_start, step_rows, 0)
        pre_act = jnp.dot(inputs_now, w_first, preferred_element_type=jnp.float32)
        activation = quick_gelu(pre_act).astype(jnp.bfloat16)
        back_grad = contract_cols(grad_now, w_second)
        pre_grad = (back_grad * quick_slope(pre_act)).astype(jnp.bfloat16)
        unit_share = contract_cols(pre_grad, w_first)
        summed = of_everyone(unit_share.astype(jnp.bfloat16), "mp").astype(jnp.float32)
        grad_prev = (grad_now.astype(jnp.float32) + summed).astype(jnp.bfloat16)
        weight = active.astype(jnp.float32)
        grad_first = grad_first + weight * contract_rows(inputs_now, pre_grad)
        grad_second = grad_second + weight * contract_rows(grad_now, activation)
        updated = lax.dynamic_update_slice_in_dim(finished, grad_prev, row_start, 0)
        finished = jnp.where(jnp.logical_and(active, is_first), updated, finished)
        if time_step + 1 < time_steps:
            incoming = shifted(grad_prev, "section", -1)
    whole_grad = picked(finished, "section", 0)
    feature_width = whole_grad.shape[1] // segment_count
    feature_start = segment_index * feature_width
    input_grad = lax.dynamic_slice_in_dim(whole_grad, feature_start, feature_width, 1)
    first_sum, second_sum = tuple(
        (
            part.astype(jnp.float32)
            for part in in_one_piece(
                (grad_first.astype(jnp.bfloat16), grad_second.astype(jnp.bfloat16)), "dp", 0, 1
            )
        )
    )
    return (image_grad, input_grad, first_sum[None], second_sum[None])


def solution(mesh):
    placed = (
        P("dp", None),
        P(("dp", "mp"), None),
        P(),
        P("section", "dp", None),
        P("section", None, "mp"),
        P("section", "mp", None),
    )
    return jax.shard_map(
        body,
        mesh=mesh,
        in_specs=placed,
        out_specs=(
            P(("dp", "mp"), None),
            P("dp", "section"),
            P("section", "dp", "mp"),
            P("section", "dp", "mp"),
        ),
        check_vma=False,
    )
```

profile of v0, /device:TPU:1, one launch (start us, length us, event | category | flops | bytes accessed | tf_op | source)
XLA Modules:
  0.0 463.0 jit_solution(3558980149796986611)
XLA Ops:
  12.4 52.9 %all-gather.3.cloned.1.call-done = bf16[4096,512]{1,0:T(8,128)(2,1)} async-done(((bf16[256,512]{1,0:T(8,128)(2,1)}), bf16[4096,512]{1,0:T(8,128)(2,1)}) %all-gather.3.cloned.1.call-update) | async-done | bytes 4194320 | tf_op jit(solution)/shard_map/all_gather | solution.py:119
  65.3 6.8 %multiply_reduce_fusion.1 = (f32[1024]{0:T(1024)S(1)}, f32[1024,4096]{1,0:T(8,128)S(1)}) fusion(f32[]{:T(128)} %bitcast.111, bf16[4096,512]{1,0:T(8,128)(2,1)} %all-gather.3.cloned.1.call-done, f32[1024]{0:T(1024)S(1)} %add_sqrt_fusion, bf16[1024,512]{1,0:T(8,128)(2,1)} %param.6), kind=kOutput, calls=%fused_computation.4 | convolution fusion | flops 4304927744 | bytes 22028292 | tf_op jit(solution)/shard_map/dot_general | solution.py:101
  82.6 8.5 %exponential_reduce_fusion = f32[4096]{0:T(1024)S(1)} fusion(f32[1024,4096]{1,0:T(8,128)} %copy-done.1, f32[4096]{0:T(1024)S(1)} %get-tuple-element.17, f32[]{:T(128)} %bitcast.115), kind=kLoop, calls=%fused_computation.1 | loop fusion | flops 12578816 | bytes 16809988 | tf_op jit(solution)/shard_map/reduce_sum | solution.py:131
  92.1 5.0 %all-to-all-start.1 = ((f32[16,2,4096]{2,1,0:T(2,128)}), f32[16,2,4096]{2,1,0:T(2,128)S(1)}, u32[]{:S(2)}, u32[]{:S(2)}) async-start(f32[16,2,4096]{2,1,0:T(2,128)} %broadcast_in_dim.51), calls=%async_computation.1 | async-start | bytes 1048576 | tf_op jit(solution)/shard_map/all_to_all | solution.py:11
  97.4 10.8 %all-to-all-done.1 = f32[16,2,4096]{2,1,0:T(2,128)S(1)} async-done(((f32[16,2,4096]{2,1,0:T(2,128)}), f32[16,2,4096]{2,1,0:T(2,128)S(1)}, u32[]{:S(2)}, u32[]{:S(2)}) %all-to-all-start.1) | async-done | bytes 524320 | tf_op jit(solution)/shard_map/all_to_all | solution.py:11
  110.7 11.4 %subtract_convert_fusion = bf16[1024,4096]{1,0:T(8,128)(2,1)S(1)} fusion(f32[1024,4096]{1,0:T(8,128)} %copy-done.1, s32[4096]{0:T(1024)S(1)} %fusion.87, f32[4096]{0:T(1024)S(1)} %bitcast.117, f32[4096]{0:T(1024)S(1)} %bitcast.118, f32[1024]{0:T(1024)S(1)} %bitcast.120, f32[1024]{0:T(1024)S(1)} %bitcast.121, f32[]{:T(128)} %bitcast.114, s32[1024]{0:T(1024)S(1)} %iota_add_fusion), kind=kLoop, calls=%fused_computation | loop fusion | flops 46137344 | bytes 25227268 | tf_op jit(solution)/shard_map/convert_element_type | solution.py:135
  132.1 6.5 %all-to-all-start.2 = ((bf16[4,1024,512]{2,1,0:T(8,128)(2,1)}), bf16[4,1024,512]{2,1,0:T(8,128)(2,1)}, u32[]{:S(2)}, u32[]{:S(2)}) async-start(bf16[4,1024,512]{2,1,0:T(8,128)(2,1)} %broadcast_in_dim.53), calls=%async_computation.3 | async-start | bytes 8388608 | tf_op jit(solution)/shard_map/all_to_all | solution.py:11
  139.0 47.0 %all-to-all-done.2 = bf16[4,1024,512]{2,1,0:T(8,128)(2,1)} async-done(((bf16[4,1024,512]{2,1,0:T(8,128)(2,1)}), bf16[4,1024,512]{2,1,0:T(8,128)(2,1)}, u32[]{:S(2)}, u32[]{:S(2)}) %all-to-all-start.2) | async-done | bytes 4194336 | tf_op jit(solution)/shard_map/all_to_all | solution.py:11
  193.7 5.2 %all-to-all-start.3 = ((bf16[4,256,512]{2,1,0:T(8,128)(2,1)}), bf16[4,256,512]{2,1,0:T(8,128)(2,1)}, u32[]{:S(2)}, u32[]{:S(2)}) async-start(bf16[4,256,512]{2,1,0:T(8,128)(2,1)} %broadcast_in_dim.55), calls=%async_computation.4 | async-start | bytes 2097152 | tf_op jit(solution)/shard_map/all_to_all | solution.py:11
  199.2 13.3 %all-to-all-done.3 = bf16[4,256,512]{2,1,0:T(8,128)(2,1)} async-done(((bf16[4,256,512]{2,1,0:T(8,128)(2,1)}), bf16[4,256,512]{2,1,0:T(8,128)(2,1)}, u32[]{:S(2)}, u32[]{:S(2)}) %all-to-all-start.3) | async-done | bytes 1048608 | tf_op jit(solution)/shard_map/all_to_all | solution.py:11
  218.2 9.9 %multiply_convert_fusion = bf16[4096,512]{1,0:T(8,128)(2,1)} fusion(bf16[1024,4096]{1,0:T(8,128)(2,1)} %copy-done.4, f32[]{:T(128)} %bitcast.110, bf16[1024,512]{1,0:T(8,128)(2,1)S(1)} %copy-done.3, f32[1024]{0:T(1024)S(1)} %add_sqrt_fusion), kind=kOutput, calls=%fused_computation.6 | convolution fusion | flops 4300734464 | bytes 13635588 | tf_op jit(solution)/shard_map/dot_general | solution.py:95
  232.9 5.2 %all-to-all-start.4 = ((bf16[4,256,512]{2,1,0:T(8,128)(2,1)}), bf16[4,256,512]{2,1,0:T(8,128)(2,1)}, u32[]{:S(2)}, u32[]{:S(2)}) async-start(bf16[4,256,512]{2,1,0:T(8,128)(2,1)} %broadcast_in_dim.56), calls=%async_computation.5 | async-start | bytes 2097152 | tf_op jit(solution)/shard_map/all_to_all | solution.py:11
  238.1 13.6 %all-to-all-done.4 = bf16[4,256,512]{2,1,0:T(8,128)(2,1)} async-done(((bf16[4,256,512]{2,1,0:T(8,128)(2,1)}), bf16[4,256,512]{2,1,0:T(8,128)(2,1)}, u32[]{:S(2)}, u32[]{:S(2)}) %all-to-all-start.4) | async-done | bytes 1048608 | tf_op jit(solution)/shard_map/all_to_all | solution.py:11
  256.6 9.9 %collective-permute-done.1 = bf16[256,512]{1,0:T(8,128)(2,1)} collective-permute-done((bf16[256,512]{1,0:T(8,128)(2,1)}, bf16[256,512]{1,0:T(8,128)(2,1)}, u32[]{:S(2)}, u32[]{:S(2)}) %collective-permute-start.1) | collective-permute-done | bytes 262176 | tf_op jit(solution)/shard_map/ppermute | solution.py:51
  271.1 5.7 %all-to-all-start.5 = ((bf16[4,256,512]{2,1,0:T(8,128)(2,1)}), bf16[4,256,512]{2,1,0:T(8,128)(2,1)}, u32[]{:S(2)}, u32[]{:S(2)}) async-start(bf16[4,256,512]{2,1,0:T(8,128)(2,1)} %broadcast_in_dim.57), calls=%async_computation.6 | async-start | bytes 2097152 | tf_op jit(solution)/shard_map/all_to_all | solution.py:11
  283.7 6.6 %all-to-all-done.5 = bf16[4,256,512]{2,1,0:T(8,128)(2,1)} async-done(((bf16[4,256,512]{2,1,0:T(8,128)(2,1)}), bf16[4,256,512]{2,1,0:T(8,128)(2,1)}, u32[]{:S(2)}, u32[]{:S(2)}) %all-to-all-start.5) | async-done | bytes 1048608 | tf_op jit(solution)/shard_map/all_to_all | solution.py:11
  297.7 6.2 %collective-permute-done.2 = bf16[256,512]{1,0:T(8,128)(2,1)S(1)} collective-permute-done((bf16[256,512]{1,0:T(8,128)(2,1)S(1)}, bf16[256,512]{1,0:T(8,128)(2,1)S(1)}, u32[]{:S(2)}, u32[]{:S(2)}) %collective-permute-start.2) | collective-permute-done | bytes 262176 | tf_op jit(solution)/shard_map/ppermute | solution.py:51
  308.4 6.0 %all-to-all-start.6 = ((bf16[4,256,512]{2,1,0:T(8,128)(2,1)}), bf16[4,256,512]{2,1,0:T(8,128)(2,1)}, u32[]{:S(2)}, u32[]{:S(2)}) async-start(bf16[4,256,512]{2,1,0:T(8,128)(2,1)} %broadcast_in_dim.58), calls=%async_computation.7 | async-start | bytes 2097152 | tf_op jit(solution)/shard_map/all_to_all | solution.py:11
  319.6 8.3 %all-to-all-done.6 = bf16[4,256,512]{2,1,0:T(8,128)(2,1)} async-done(((bf16[4,256,512]{2,1,0:T(8,128)(2,1)}), bf16[4,256,512]{2,1,0:T(8,128)(2,1)}, u32[]{:S(2)}, u32[]{:S(2)}) %all-to-all-start.6) | async-done | bytes 1048608 | tf_op jit(solution)/shard_map/all_to_all | solution.py:11
  334.1 7.5 %collective-permute-done.3 = bf16[256,512]{1,0:T(8,128)(2,1)S(1)} collective-permute-done((bf16[256,512]{1,0:T(8,128)(2,1)S(1)}, bf16[256,512]{1,0:T(8,128)(2,1)S(1)}, u32[]{:S(2)}, u32[]{:S(2)}) %collective-permute-start.3) | collective-permute-done | bytes 262176 | tf_op jit(solution)/shard_map/ppermute | solution.py:51
  348.5 5.3 %all-to-all-start.7 = ((bf16[4,256,512]{2,1,0:T(8,128)(2,1)}), bf16[4,256,512]{2,1,0:T(8,128)(2,1)S(1)}, u32[]{:S(2)}, u32[]{:S(2)}) async-start(bf16[4,256,512]{2,1,0:T(8,128)(2,1)} %broadcast_in_dim.59), calls=%async_computation.8 | async-start | bytes 2097152 | tf_op jit(solution)/shard_map/all_to_all | solution.py:11
  356.0 11.3 %all-to-all-done.7 = bf16[4,256,512]{2,1,0:T(8,128)(2,1)S(1)} async-done(((bf16[4,256,512]{2,1,0:T(8,128)(2,1)}), bf16[4,256,512]{2,1,0:T(8,128)(2,1)S(1)}, u32[]{:S(2)}, u32[]{:S(2)}) %all-to-all-start.7) | async-done | bytes 1048608 | tf_op jit(solution)/shard_map/all_to_all | solution.py:11
  372.4 42.6 %reduce-scatter.7.cloned.1.call-done = bf16[32,1024]{1,0:T(8,128)(2,1)} async-done(((bf16[512,1024]{1,0:T(8,128)(2,1)}), bf16[32,1024]{1,0:T(8,128)(2,1)}) %reduce-scatter.7.cloned.1.call-update) | async-done | bytes 65552
  417.5 36.8 %all-gather.5.cloned.1.call-done = bf16[2,1024,512]{2,1,0:T(8,128)(2,1)} async-done(((bf16[1,1024,512]{2,1,0:T(8,128)(2,1)}), bf16[2,1024,512]{2,1,0:T(8,128)(2,1)}) %all-gather.5.cloned.1.call-update) | async-done | bytes 2097168 | tf_op jit(solution)/shard_map/all_gather | solution.py:55
  (166 shorter events, 105.5 us)
Async XLA Ops:
  7.2 131.5 %copy-start = (bf16[1,1024,512]{2,1,0:T(8,128)(2,1)S(1)}, bf16[1,1024,512]{2,1,0:T(8,128)(2,1)}, u32[]{:S(2)}) copy-start(bf16[1,1024,512]{2,1,0:T(8,128)(2,1)} %param.9) | copy-start | bytes 3145732
  7.2 58.1 %all-gather.3.cloned.1.call-start = ((), (), s32[]{:S(2)}) async-start(), calls=%async_computation.10 | async-start | bytes 4456448 | tf_op jit(solution)/shard_map/all_gather | solution.py:119
  78.5 12.6 %all-to-all-start = ((f32[4,2,1024]{2,1,0:T(2,128)}), f32[4,2,1024]{2,1,0:T(2,128)S(1)}, u32[]{:S(2)}, u32[]{:S(2)}) async-start(f32[4,2,1024]{2,1,0:T(2,128)} %broadcast_in_dim.50), calls=%async_computation | async-start | bytes 65536 | tf_op jit(solution)/shard_map/all_to_all | solution.py:11
  92.1 16.0 %all-to-all-start.1 = ((f32[16,2,4096]{2,1,0:T(2,128)}), f32[16,2,4096]{2,1,0:T(2,128)S(1)}, u32[]{:S(2)}, u32[]{:S(2)}) async-start(f32[16,2,4096]{2,1,0:T(2,128)} %broadcast_in_dim.51), calls=%async_computation.1 | async-start | bytes 1048576 | tf_op jit(solution)/shard_map/all_to_all | solution.py:11
  132.1 57.0 %copy-start.3 = (bf16[1024,512]{1,0:T(8,128)(2,1)S(1)}, bf16[1024,512]{1,0:T(8,128)(2,1)}, u32[]{:S(2)}) copy-start(bf16[1024,512]{1,0:T(8,128)(2,1)} %param.6) | copy-start | bytes 3145732
  132.1 53.8 %all-to-all-start.2 = ((bf16[4,1024,512]{2,1,0:T(8,128)(2,1)}), bf16[4,1024,512]{2,1,0:T(8,128)(2,1)}, u32[]{:S(2)}, u32[]{:S(2)}) async-start(bf16[4,1024,512]{2,1,0:T(8,128)(2,1)} %broadcast_in_dim.53), calls=%async_computation.3 | async-start | bytes 8388608 | tf_op jit(solution)/shard_map/all_to_all | solution.py:11
  139.0 52.6 %copy-start.19 = (f32[256,512]{1,0:T(8,128)}, f32[256,512]{1,0:T(8,128)S(1)}, u32[]{:S(2)}) copy-start(f32[256,512]{1,0:T(8,128)S(1)} %fusion.33) | copy-start | bytes 1572868
  193.7 18.8 %all-to-all-start.3 = ((bf16[4,256,512]{2,1,0:T(8,128)(2,1)}), bf16[4,256,512]{2,1,0:T(8,128)(2,1)}, u32[]{:S(2)}, u32[]{:S(2)}) async-start(bf16[4,256,512]{2,1,0:T(8,128)(2,1)} %broadcast_in_dim.55), calls=%async_computation.4 | async-start | bytes 2097152 | tf_op jit(solution)/shard_map/all_to_all | solution.py:11
  198.9 170.4 %reduce-scatter.5.cloned.1.call-start = ((), (), s32[]{:S(2)}) async-start(), calls=%async_computation.11 | async-start | bytes 4456448 | tf_op jit(solution)/shard_map/reduce_scatter | solution.py:139
  199.2 30.1 %copy-start.20 = (f32[256,512]{1,0:T(8,128)}, f32[256,512]{1,0:T(8,128)S(1)}, u32[]{:S(2)}) copy-start(f32[256,512]{1,0:T(8,128)S(1)} %fusion.30) | copy-start | bytes 1572868
  216.7 11.4 %collective-permute-start = (bf16[256,512]{1,0:T(8,128)(2,1)S(1)}, bf16[256,512]{1,0:T(8,128)(2,1)}, u32[]{:S(2)}, u32[]{:S(2)}) collective-permute-start(bf16[256,512]{1,0:T(8,128)(2,1)S(1)} %get-tuple-element.25), channel_id=1, source_target_pairs={{64,0},{65,1},{66,2},{67,3},{68,4},{69,5},{70,6},{71,7},{72,8},{73... | collective-permute-start | bytes 786440 | tf_op jit(solution)/shard_map/ppermute | solution.py:51
  228.1 38.4 %copy-start.6 = (bf16[1024,512]{1,0:T(8,128)(2,1)S(1)}, bf16[1024,512]{1,0:T(8,128)(2,1)}, u32[]{:S(2)}) copy-start(bf16[1024,512]{1,0:T(8,128)(2,1)} %copy-done.5) | copy-start | bytes 3145732
  229.3 27.3 %copy-start.14 = (bf16[256,512]{1,0:T(8,128)(2,1)}, bf16[256,512]{1,0:T(8,128)(2,1)S(1)}, u32[]{:S(2)}) copy-start(bf16[256,512]{1,0:T(8,128)(2,1)S(1)} %slice_select_fusion.1) | copy-start | bytes 786436
  232.9 18.7 %all-to-all-start.4 = ((bf16[4,256,512]{2,1,0:T(8,128)(2,1)}), bf16[4,256,512]{2,1,0:T(8,128)(2,1)}, u32[]{:S(2)}, u32[]{:S(2)}) async-start(bf16[4,256,512]{2,1,0:T(8,128)(2,1)} %broadcast_in_dim.56), calls=%async_computation.5 | async-start | bytes 2097152 | tf_op jit(solution)/shard_map/all_to_all | solution.py:11
  255.0 11.5 %collective-permute-start.1 = (bf16[256,512]{1,0:T(8,128)(2,1)}, bf16[256,512]{1,0:T(8,128)(2,1)}, u32[]{:S(2)}, u32[]{:S(2)}) collective-permute-start(bf16[256,512]{1,0:T(8,128)(2,1)} %get-tuple-element.23), channel_id=1, source_target_pairs={{64,0},{65,1},{66,2},{67,3},{68,4},{69,5},{70,6},{71,7},{72,8},{73... | collective-permute-start | bytes 786440 | tf_op jit(solution)/shard_map/ppermute | solution.py:51
  271.1 19.3 %all-to-all-start.5 = ((bf16[4,256,512]{2,1,0:T(8,128)(2,1)}), bf16[4,256,512]{2,1,0:T(8,128)(2,1)}, u32[]{:S(2)}, u32[]{:S(2)}) async-start(bf16[4,256,512]{2,1,0:T(8,128)(2,1)} %broadcast_in_dim.57), calls=%async_computation.6 | async-start | bytes 2097152 | tf_op jit(solution)/shard_map/all_to_all | solution.py:11
  293.6 10.3 %collective-permute-start.2 = (bf16[256,512]{1,0:T(8,128)(2,1)S(1)}, bf16[256,512]{1,0:T(8,128)(2,1)S(1)}, u32[]{:S(2)}, u32[]{:S(2)}) collective-permute-start(bf16[256,512]{1,0:T(8,128)(2,1)S(1)} %get-tuple-element.21), channel_id=1, source_target_pairs={{64,0},{65,1},{66,2},{67,3},{68,4},{69,5},{70,6},{71,7},{72,8},{73... | collective-permute-start | bytes 786440 | tf_op jit(solution)/shard_map/ppermute | solution.py:51
  308.4 19.6 %all-to-all-start.6 = ((bf16[4,256,512]{2,1,0:T(8,128)(2,1)}), bf16[4,256,512]{2,1,0:T(8,128)(2,1)}, u32[]{:S(2)}, u32[]{:S(2)}) async-start(bf16[4,256,512]{2,1,0:T(8,128)(2,1)} %broadcast_in_dim.58), calls=%async_computation.7 | async-start | bytes 2097152 | tf_op jit(solution)/shard_map/all_to_all | solution.py:11
  314.3 100.6 %reduce-scatter.7.cloned.1.call-start = ((), (), s32[]{:S(2)}) async-start(), calls=%async_computation.13 | async-start | bytes 1114112
  331.3 10.3 %collective-permute-start.3 = (bf16[256,512]{1,0:T(8,128)(2,1)S(1)}, bf16[256,512]{1,0:T(8,128)(2,1)S(1)}, u32[]{:S(2)}, u32[]{:S(2)}) collective-permute-start(bf16[256,512]{1,0:T(8,128)(2,1)S(1)} %get-tuple-element.19), channel_id=1, source_target_pairs={{64,0},{65,1},{66,2},{67,3},{68,4},{69,5},{70,6},{71,7},{72,8},{73... | collective-permute-start | bytes 786440 | tf_op jit(solution)/shard_map/ppermute | solution.py:51
  344.6 22.9 %copy-start.16 = (bf16[256,512]{1,0:T(8,128)(2,1)S(1)}, bf16[256,512]{1,0:T(8,128)(2,1)}, u32[]{:S(2)}) copy-start(bf16[256,512]{1,0:T(8,128)(2,1)} %copy-done.15) | copy-start | bytes 786436
  344.6 24.7 %copy-start.8 = (bf16[256,512]{1,0:T(8,128)(2,1)S(1)}, bf16[256,512]{1,0:T(8,128)(2,1)}, u32[]{:S(2)}) copy-start(bf16[256,512]{1,0:T(8,128)(2,1)} %param.7) | copy-start | bytes 786436
  348.5 18.9 %all-to-all-start.7 = ((bf16[4,256,512]{2,1,0:T(8,128)(2,1)}), bf16[4,256,512]{2,1,0:T(8,128)(2,1)S(1)}, u32[]{:S(2)}, u32[]{:S(2)}) async-start(bf16[4,256,512]{2,1,0:T(8,128)(2,1)} %broadcast_in_dim.59), calls=%async_computation.8 | async-start | bytes 2097152 | tf_op jit(solution)/shard_map/all_to_all | solution.py:11
  353.8 100.5 %all-gather.5.cloned.1.call-start = ((), (), s32[]{:S(2)}) async-start(), calls=%async_computation.12 | async-start | bytes 3145728 | tf_op jit(solution)/shard_map/all_gather | solution.py:55
  (16 other events, 93.0 us)
Sparse Core Ops, SparseCore 0:
  10.7 54.5 all-gather.2
  228.2 76.3 reduce-scatter.4
  346.2 68.7 reduce-scatter.6
  416.4 37.8 all-gather.4
where the time goes:
time: 465 us; the launch traced here: 463 us
  waiting for transfers between devices  267 us (57%)
  other arithmetic  53.6 us (12%)
  matrix products  49 us (11%)
  starting transfers between devices  48.3 us (10%)
  local copies, waits for them, and re-layouts  30 us (6%)
  between operations  15.2 us (3%)
    all_to_all x8, waiting for transfers between devices, from_everyone(): return lax.all_to_all(copies, axis, split_axis=0, concat_axis=0, tiled=True)  111 us
    all_gather x1, waiting for transfers between devices, body(): columns = lax.all_gather(image_low, 'dp', axis=0, tiled=True)  52.9 us
    all_to_all x8, starting transfers between devices, from_everyone(): return lax.all_to_all(copies, axis, split_axis=0, concat_axis=0, tiled=True)  42.9 us
    unnamed x5, waiting for transfers between devices  42.6 us
    all_gather x1, waiting for transfers between devices, picked(): lax.all_gather(array, axis)  36.8 us
    dot_general x11, matrix products, contract_rows(): lax.dot_general(left_side, right_side, (((0,), (0,)), ((), ())), preferre...  25.3 us
    ppermute x4, waiting for transfers between devices, shifted(): return lax.ppermute(block, axis, route)  23.6 us
    dot_general x11, matrix products, contract_cols(): lax.dot_general(left_side, right_side, (((1,), (1,)), ((), ())), preferre...  16.1 us
  transfers between devices with their start and end apart: 16, of which 13 were waited for; matrix products, arithmetic and copies ran while one was open for 16% of the time, Pallas kernels for 0%

commit v1 on v0

--- a/solution.py
+++ b/solution.py
@@ -4,6 +4,42 @@
 from jax.sharding import PartitionSpec as P
 
 MICRO = 4
+
+
+def check_surface(field_in):
+    a_name = "dp"
+    u_next = lax.psum(1, a_name)
+    far_arr = lax.axis_index(a_name)
+    upper, current_arr, piece_now = (u_next, far_arr, field_in.shape[0])
+    frames = []
+    for it, num in enumerate(field_in.shape):
+        frames.append(num * upper if it == 0 else num)
+    z_new = jnp.zeros(frames, field_in.dtype)
+    prior = lax.dynamic_update_slice_in_dim(z_new, field_in, current_arr * piece_now, axis=0)
+    answer = new = field_in
+    u = 1
+    while u < upper // 2 + 1:
+        steps_seen = []
+        it = 0
+        while it < upper:
+            steps_seen.append((it, (it + 1) % upper))
+            it += 1
+        answer = lax.ppermute(answer, a_name, perm=steps_seen)
+        prior = lax.dynamic_update_slice_in_dim(
+            prior, answer, (current_arr - u) % upper * piece_now, axis=0
+        )
+        if 2 * u < upper:
+            by_place = []
+            it = 0
+            while it < upper:
+                by_place.append((it, (it - 1) % upper))
+                it += 1
+            new = lax.ppermute(new, a_name, perm=by_place)
+            prior = lax.dynamic_update_slice_in_dim(
+                prior, new, (current_arr + u) % upper * piece_now, axis=0
+            )
+        u = u + 1
+    return prior
 
 
 def from_everyone(array, axis):
@@ -116,7 +152,7 @@
     image_unit, image_length = unit_rows(image_feats)
     text_low = text_unit.astype(jnp.bfloat16)
     image_low = image_unit.astype(jnp.bfloat16)
-    columns = lax.all_gather(image_low, "dp", axis=0, tiled=True)
+    columns = check_surface(image_low)
     column_total_count = columns.shape[0]
     scores = logit_mult * contract_cols(text_low, columns)
     text_ids = dp_index * row_count + jnp.arange(row_count, dtype=jnp.int32)

time: 465 us -> 468 us (level)
  the two profiles are of different devices: /device:TPU:1 before, /device:TPU:0 now
where the time goes in v1:
time: 468 us; the launch traced here: 459 us
  waiting for transfers between devices  218 us (47%)
  starting transfers between devices  78.1 us (17%)
  other arithmetic  50.1 us (11%)
  local copies, waits for them, and re-layouts  47.5 us (10%)
  matrix products  47.3 us (10%)
  between operations  17.3 us (4%)
    all_to_all x8, waiting for transfers between devices, from_everyone(): return lax.all_to_all(copies, axis, split_axis=0, concat_axis=0, tiled=True)  117 us
    unnamed x4, waiting for transfers between devices  45.2 us
    ppermute x7, starting transfers between devices, check_surface(): new = lax.ppermute(new, a_name, perm=by_place)  37.9 us
    all_to_all x8, starting transfers between devices, from_everyone(): return lax.all_to_all(copies, axis, split_axis=0, concat_axis=0, tiled=True)  33 us
    ppermute x8, waiting for transfers between devices, check_surface(): answer = lax.ppermute(answer, a_name, perm=steps_seen)  29.3 us
    ppermute x4, waiting for transfers between devices, shifted(): return lax.ppermute(block, axis, route)  25.4 us
    dot_general x11, matrix products, contract_rows(): lax.dot_general(left_side, right_side, (((0,), (0,)), ((), ())), preferre...  24.3 us
    unnamed x62, local copies, waits for them, and re-layouts  16 us
  transfers between devices with their start and end apart: 30, of which 21 were waited for; matrix products, arithmetic and copies ran while one was open for 18% of the time, Pallas kernels for 0%

profile of v1, /device:TPU:0, one launch (start us, length us, event | category | flops | bytes accessed | tf_op | source)
XLA Modules:
  0.0 458.5 jit_solution(12900573784471223156)
XLA Ops:
  19.0 6.3 %collective-permute-done = bf16[256,512]{1,0:T(8,128)(2,1)S(1)} collective-permute-done((bf16[256,512]{1,0:T(8,128)(2,1)S(1)}, bf16[256,512]{1,0:T(8,128)(2,1)S(1)}, u32[]{:S(2)}, u32[]{:S(2)}) %collective-permute-start) | collective-permute-done | bytes 262176 | tf_op jit(solution)/shard_map/ppermute | solution.py:27
  25.3 5.3 %collective-permute-start.3 = (bf16[256,512]{1,0:T(8,128)(2,1)S(1)}, bf16[256,512]{1,0:T(8,128)(2,1)S(1)}, u32[]{:S(2)}, u32[]{:S(2)}) collective-permute-start(bf16[256,512]{1,0:T(8,128)(2,1)S(1)} %collective-permute-done.1), channel_id=1, source_target_pairs={{0,60},{4,0},{8,4},{12,8},{16,12},{20,16},{24,20},{28,24},{32,28},... | collective-permute-start | bytes 786440 | tf_op jit(solution)/shard_map/ppermute | solution.py:37
  36.1 5.4 %collective-permute-start.5 = (bf16[256,512]{1,0:T(8,128)(2,1)S(1)}, bf16[256,512]{1,0:T(8,128)(2,1)S(1)}, u32[]{:S(2)}, u32[]{:S(2)}) collective-permute-start(bf16[256,512]{1,0:T(8,128)(2,1)S(1)} %collective-permute-done.3), channel_id=1, source_target_pairs={{0,60},{4,0},{8,4},{12,8},{16,12},{20,16},{24,20},{28,24},{32,28},... | collective-permute-start | bytes 786440 | tf_op jit(solution)/shard_map/ppermute | solution.py:37
  48.5 5.3 %collective-permute-start.7 = (bf16[256,512]{1,0:T(8,128)(2,1)S(1)}, bf16[256,512]{1,0:T(8,128)(2,1)S(1)}, u32[]{:S(2)}, u32[]{:S(2)}) collective-permute-start(bf16[256,512]{1,0:T(8,128)(2,1)S(1)} %collective-permute-done.5), channel_id=1, source_target_pairs={{0,60},{4,0},{8,4},{12,8},{16,12},{20,16},{24,20},{28,24},{32,28},... | collective-permute-start | bytes 786440 | tf_op jit(solution)/shard_map/ppermute | solution.py:37
  57.7 5.8 %collective-permute-start.9 = (bf16[256,512]{1,0:T(8,128)(2,1)S(1)}, bf16[256,512]{1,0:T(8,128)(2,1)S(1)}, u32[]{:S(2)}, u32[]{:S(2)}) collective-permute-start(bf16[256,512]{1,0:T(8,128)(2,1)S(1)} %collective-permute-done.7), channel_id=1, source_target_pairs={{0,60},{4,0},{8,4},{12,8},{16,12},{20,16},{24,20},{28,24},{32,28},... | collective-permute-start | bytes 786440 | tf_op jit(solution)/shard_map/ppermute | solution.py:37
  68.5 5.3 %collective-permute-start.11 = (bf16[256,512]{1,0:T(8,128)(2,1)S(1)}, bf16[256,512]{1,0:T(8,128)(2,1)S(1)}, u32[]{:S(2)}, u32[]{:S(2)}) collective-permute-start(bf16[256,512]{1,0:T(8,128)(2,1)S(1)} %collective-permute-done.9), channel_id=1, source_target_pairs={{0,60},{4,0},{8,4},{12,8},{16,12},{20,16},{24,20},{28,24},{32,28},... | collective-permute-start | bytes 786440 | tf_op jit(solution)/shard_map/ppermute | solution.py:37
  77.9 5.8 %collective-permute-start.13 = (bf16[256,512]{1,0:T(8,128)(2,1)S(1)}, bf16[256,512]{1,0:T(8,128)(2,1)S(1)}, u32[]{:S(2)}, u32[]{:S(2)}) collective-permute-start(bf16[256,512]{1,0:T(8,128)(2,1)S(1)} %collective-permute-done.11), channel_id=1, source_target_pairs={{0,60},{4,0},{8,4},{12,8},{16,12},{20,16},{24,20},{28,24},{32,28},... | collective-permute-start | bytes 786440 | tf_op jit(solution)/shard_map/ppermute | solution.py:37
  88.7 7.5 %collective-permute-done.14 = bf16[256,512]{1,0:T(8,128)(2,1)S(1)} collective-permute-done((bf16[256,512]{1,0:T(8,128)(2,1)S(1)}, bf16[256,512]{1,0:T(8,128)(2,1)S(1)}, u32[]{:S(2)}, u32[]{:S(2)}) %collective-permute-start.14) | collective-permute-done | bytes 262176 | tf_op jit(solution)/shard_map/ppermute | solution.py:27
  97.0 6.6 %multiply_reduce_fusion.1 = (f32[1024]{0:T(1024)S(1)}, f32[1024,4096]{1,0:T(8,128)S(1)}) fusion(f32[]{:T(128)} %bitcast.111, bf16[4096,512]{1,0:T(8,128)(2,1)} %constant_dynamic-update-slice_fusion, f32[1024]{0:T(1024)S(1)} %add_sqrt_fusion, bf16[1024,512]{1,0:T(8,128)(2,1)S(1)} %copy-done.3), kind=kOutput, calls=%fused_computation.4 | convolution fusion | flops 4304927744 | bytes 22028292 | tf_op jit(solution)/shard_map/dot_general | solution.py:137
  113.7 8.5 %exponential_reduce_fusion = f32[4096]{0:T(1024)S(1)} fusion(f32[1024,4096]{1,0:T(8,128)} %copy-done.1, f32[4096]{0:T(1024)S(1)} %get-tuple-element.17, f32[]{:T(128)} %bitcast.115), kind=kLoop, calls=%fused_computation.1 | loop fusion | flops 12578816 | bytes 16809988 | tf_op jit(solution)/shard_map/reduce_sum | solution.py:167
  127.1 12.2 %all-to-all-done.1 = f32[16,2,4096]{2,1,0:T(2,128)S(1)} async-done(((f32[16,2,4096]{2,1,0:T(2,128)}), f32[16,2,4096]{2,1,0:T(2,128)S(1)}, u32[]{:S(2)}, u32[]{:S(2)}) %all-to-all-start.1) | async-done | bytes 524320 | tf_op jit(solution)/shard_map/all_to_all | solution.py:47
  141.8 11.3 %subtract_convert_fusion = bf16[1024,4096]{1,0:T(8,128)(2,1)S(1)} fusion(f32[1024,4096]{1,0:T(8,128)} %copy-done.1, s32[4096]{0:T(1024)S(1)} %fusion.87, f32[4096]{0:T(1024)S(1)} %bitcast.117, f32[4096]{0:T(1024)S(1)} %bitcast.118, f32[1024]{0:T(1024)S(1)} %bitcast.120, f32[1024]{0:T(1024)S(1)} %bitcast.121, f32[]{:T(128)} %bitcast.114, s32[1024]{0:T(1024)S(1)} %iota_add_fusion), kind=kLoop, calls=%fused_computation | loop fusion | flops 46137344 | bytes 25227268 | tf_op jit(solution)/shard_map/convert_element_type | solution.py:171
  156.3 6.7 %multiply_convert_fusion.1 = bf16[1024,512]{1,0:T(8,128)(2,1)S(1)} fusion(bf16[1024,4096]{1,0:T(8,128)(2,1)S(1)} %subtract_convert_fusion, bf16[4096,512]{1,0:T(8,128)(2,1)} %constant_dynamic-update-slice_fusion, f32[]{:T(128)} %bitcast.112), kind=kOutput, calls=%fused_computation.17 | convolution fusion | flops 4296015872 | bytes 13631492 | tf_op jit(solution)/shard_map/dot_general | solution.py:172
  170.7 47.8 %all-to-all-done.2 = bf16[4,1024,512]{2,1,0:T(8,128)(2,1)} async-done(((bf16[4,1024,512]{2,1,0:T(8,128)(2,1)}), bf16[4,1024,512]{2,1,0:T(8,128)(2,1)}, u32[]{:S(2)}, u32[]{:S(2)}) %all-to-all-start.2) | async-done | bytes 4194336 | tf_op jit(solution)/shard_map/all_to_all | solution.py:47
  231.7 13.3 %all-to-all-done.3 = bf16[4,256,512]{2,1,0:T(8,128)(2,1)} async-done(((bf16[4,256,512]{2,1,0:T(8,128)(2,1)}), bf16[4,256,512]{2,1,0:T(8,128)(2,1)}, u32[]{:S(2)}, u32[]{:S(2)}) %all-to-all-start.3) | async-done | bytes 1048608 | tf_op jit(solution)/shard_map/all_to_all | solution.py:47
  250.5 9.9 %multiply_convert_fusion = bf16[4096,512]{1,0:T(8,128)(2,1)} fusion(bf16[1024,4096]{1,0:T(8,128)(2,1)} %copy-done.4, f32[]{:T(128)} %bitcast.110, bf16[1024,512]{1,0:T(8,128)(2,1)S(1)} %copy-done.3, f32[1024]{0:T(1024)S(1)} %add_sqrt_fusion), kind=kOutput, calls=%fused_computation.6 | convolution fusion | flops 4300734464 | bytes 13635588 | tf_op jit(solution)/shard_map/dot_general | solution.py:131
  269.6 14.5 %all-to-all-done.4 = bf16[4,256,512]{2,1,0:T(8,128)(2,1)} async-done(((bf16[4,256,512]{2,1,0:T(8,128)(2,1)}), bf16[4,256,512]{2,1,0:T(8,128)(2,1)}, u32[]{:S(2)}, u32[]{:S(2)}) %all-to-all-start.4) | async-done | bytes 1048608 | tf_op jit(solution)/shard_map/all_to_all | solution.py:47
  289.0 9.9 %collective-permute-done.16 = bf16[256,512]{1,0:T(8,128)(2,1)} collective-permute-done((bf16[256,512]{1,0:T(8,128)(2,1)S(1)}, bf16[256,512]{1,0:T(8,128)(2,1)}, u32[]{:S(2)}, u32[]{:S(2)}) %collective-permute-start.16) | collective-permute-done | bytes 262176 | tf_op jit(solution)/shard_map/ppermute | solution.py:87
  314.7 7.6 %all-to-all-done.5 = bf16[4,256,512]{2,1,0:T(8,128)(2,1)} async-done(((bf16[4,256,512]{2,1,0:T(8,128)(2,1)}), bf16[4,256,512]{2,1,0:T(8,128)(2,1)}, u32[]{:S(2)}, u32[]{:S(2)}) %all-to-all-start.5) | async-done | bytes 1048608 | tf_op jit(solution)/shard_map/all_to_all | solution.py:47
  329.7 7.0 %collective-permute-done.17 = bf16[256,512]{1,0:T(8,128)(2,1)S(1)} collective-permute-done((bf16[256,512]{1,0:T(8,128)(2,1)S(1)}, bf16[256,512]{1,0:T(8,128)(2,1)S(1)}, u32[]{:S(2)}, u32[]{:S(2)}) %collective-permute-start.17) | collective-permute-done | bytes 262176 | tf_op jit(solution)/shard_map/ppermute | solution.py:87
  348.9 9.9 %all-to-all-done.6 = bf16[4,256,512]{2,1,0:T(8,128)(2,1)} async-done(((bf16[4,256,512]{2,1,0:T(8,128)(2,1)}), bf16[4,256,512]{2,1,0:T(8,128)(2,1)}, u32[]{:S(2)}, u32[]{:S(2)}) %all-to-all-start.6) | async-done | bytes 1048608 | tf_op jit(solution)/shard_map/all_to_all | solution.py:47
  364.8 8.4 %collective-permute-done.18 = bf16[256,512]{1,0:T(8,128)(2,1)S(1)} collective-permute-done((bf16[256,512]{1,0:T(8,128)(2,1)S(1)}, bf16[256,512]{1,0:T(8,128)(2,1)S(1)}, u32[]{:S(2)}, u32[]{:S(2)}) %collective-permute-start.18) | collective-permute-done | bytes 262176 | tf_op jit(solution)/shard_map/ppermute | solution.py:87
  383.9 12.0 %all-to-all-done.7 = bf16[4,256,512]{2,1,0:T(8,128)(2,1)S(1)} async-done(((bf16[4,256,512]{2,1,0:T(8,128)(2,1)}), bf16[4,256,512]{2,1,0:T(8,128)(2,1)S(1)}, u32[]{:S(2)}, u32[]{:S(2)}) %all-to-all-start.7) | async-done | bytes 1048608 | tf_op jit(solution)/shard_map/all_to_all | solution.py:47
  401.0 45.2 %reduce-scatter.7.cloned.1.call-done = bf16[32,1024]{1,0:T(8,128)(2,1)} async-done(((bf16[512,1024]{1,0:T(8,128)(2,1)}), bf16[32,1024]{1,0:T(8,128)(2,1)}) %reduce-scatter.7.cloned.1.call-update) | async-done | bytes 65552
  (217 shorter events, 163.5 us)
Async XLA Ops:
  12.4 12.9 %collective-permute-start = (bf16[256,512]{1,0:T(8,128)(2,1)S(1)}, bf16[256,512]{1,0:T(8,128)(2,1)S(1)}, u32[]{:S(2)}, u32[]{:S(2)}) collective-permute-start(bf16[256,512]{1,0:T(8,128)(2,1)S(1)} %get-tuple-element.39), channel_id=1, source_target_pairs={{0,4},{4,8},{8,12},{12,16},{16,20},{20,24},{24,28},{28,32},{32,36}... | collective-permute-start | bytes 786440 | tf_op jit(solution)/shard_map/ppermute | solution.py:27
  14.1 11.2 %collective-permute-start.1 = (bf16[256,512]{1,0:T(8,128)(2,1)S(1)}, bf16[256,512]{1,0:T(8,128)(2,1)S(1)}, u32[]{:S(2)}, u32[]{:S(2)}) collective-permute-start(bf16[256,512]{1,0:T(8,128)(2,1)S(1)} %get-tuple-element.39), channel_id=1, source_target_pairs={{0,60},{4,0},{8,4},{12,8},{16,12},{20,16},{24,20},{28,24},{32,28},... | collective-permute-start | bytes 786440 | tf_op jit(solution)/shard_map/ppermute | solution.py:37
  25.3 10.8 %collective-permute-start.2 = (bf16[256,512]{1,0:T(8,128)(2,1)S(1)}, bf16[256,512]{1,0:T(8,128)(2,1)S(1)}, u32[]{:S(2)}, u32[]{:S(2)}) collective-permute-start(bf16[256,512]{1,0:T(8,128)(2,1)S(1)} %collective-permute-done), channel_id=1, source_target_pairs={{0,4},{4,8},{8,12},{12,16},{16,20},{20,24},{24,28},{28,32},{32,36}... | collective-permute-start | bytes 786440 | tf_op jit(solution)/shard_map/ppermute | solution.py:27
  25.3 10.8 %collective-permute-start.3 = (bf16[256,512]{1,0:T(8,128)(2,1)S(1)}, bf16[256,512]{1,0:T(8,128)(2,1)S(1)}, u32[]{:S(2)}, u32[]{:S(2)}) collective-permute-start(bf16[256,512]{1,0:T(8,128)(2,1)S(1)} %collective-permute-done.1), channel_id=1, source_target_pairs={{0,60},{4,0},{8,4},{12,8},{16,12},{20,16},{24,20},{28,24},{32,28},... | collective-permute-start | bytes 786440 | tf_op jit(solution)/shard_map/ppermute | solution.py:37
  36.1 10.0 %collective-permute-start.4 = (bf16[256,512]{1,0:T(8,128)(2,1)S(1)}, bf16[256,512]{1,0:T(8,128)(2,1)}, u32[]{:S(2)}, u32[]{:S(2)}) collective-permute-start(bf16[256,512]{1,0:T(8,128)(2,1)S(1)} %collective-permute-done.2), channel_id=1, source_target_pairs={{0,4},{4,8},{8,12},{12,16},{16,20},{20,24},{24,28},{28,32},{32,36}... | collective-permute-start | bytes 786440 | tf_op jit(solution)/shard_map/ppermute | solution.py:27
  36.1 12.4 %collective-permute-start.5 = (bf16[256,512]{1,0:T(8,128)(2,1)S(1)}, bf16[256,512]{1,0:T(8,128)(2,1)S(1)}, u32[]{:S(2)}, u32[]{:S(2)}) collective-permute-start(bf16[256,512]{1,0:T(8,128)(2,1)S(1)} %collective-permute-done.3), channel_id=1, source_target_pairs={{0,60},{4,0},{8,4},{12,8},{16,12},{20,16},{24,20},{28,24},{32,28},... | collective-permute-start | bytes 786440 | tf_op jit(solution)/shard_map/ppermute | solution.py:37
  57.7 10.7 %collective-permute-start.9 = (bf16[256,512]{1,0:T(8,128)(2,1)S(1)}, bf16[256,512]{1,0:T(8,128)(2,1)S(1)}, u32[]{:S(2)}, u32[]{:S(2)}) collective-permute-start(bf16[256,512]{1,0:T(8,128)(2,1)S(1)} %collective-permute-done.7), channel_id=1, source_target_pairs={{0,60},{4,0},{8,4},{12,8},{16,12},{20,16},{24,20},{28,24},{32,28},... | collective-permute-start | bytes 786440 | tf_op jit(solution)/shard_map/ppermute | solution.py:37
  75.7 10.8 %collective-permute-start.12 = (bf16[256,512]{1,0:T(8,128)(2,1)S(1)}, bf16[256,512]{1,0:T(8,128)(2,1)S(1)}, u32[]{:S(2)}, u32[]{:S(2)}) collective-permute-start(bf16[256,512]{1,0:T(8,128)(2,1)S(1)} %collective-permute-done.10), channel_id=1, source_target_pairs={{0,4},{4,8},{8,12},{12,16},{16,20},{20,24},{24,28},{28,32},{32,36}... | collective-permute-start | bytes 786440 | tf_op jit(solution)/shard_map/ppermute | solution.py:27
  77.9 10.1 %collective-permute-start.13 = (bf16[256,512]{1,0:T(8,128)(2,1)S(1)}, bf16[256,512]{1,0:T(8,128)(2,1)S(1)}, u32[]{:S(2)}, u32[]{:S(2)}) collective-permute-start(bf16[256,512]{1,0:T(8,128)(2,1)S(1)} %collective-permute-done.11), channel_id=1, source_target_pairs={{0,60},{4,0},{8,4},{12,8},{16,12},{20,16},{24,20},{28,24},{32,28},... | collective-permute-start | bytes 786440 | tf_op jit(solution)/shard_map/ppermute | solution.py:37
  109.9 12.3 %all-to-all-start = ((f32[4,2,1024]{2,1,0:T(2,128)}), f32[4,2,1024]{2,1,0:T(2,128)S(1)}, u32[]{:S(2)}, u32[]{:S(2)}) async-start(f32[4,2,1024]{2,1,0:T(2,128)} %broadcast_in_dim.54), calls=%async_computation | async-start | bytes 65536 | tf_op jit(solution)/shard_map/all_to_all | solution.py:47
  123.2 16.0 %all-to-all-start.1 = ((f32[16,2,4096]{2,1,0:T(2,128)}), f32[16,2,4096]{2,1,0:T(2,128)S(1)}, u32[]{:S(2)}, u32[]{:S(2)}) async-start(f32[16,2,4096]{2,1,0:T(2,128)} %broadcast_in_dim.55), calls=%async_computation.1 | async-start | bytes 1048576 | tf_op jit(solution)/shard_map/all_to_all | solution.py:47
  165.2 53.3 %all-to-all-start.2 = ((bf16[4,1024,512]{2,1,0:T(8,128)(2,1)}), bf16[4,1024,512]{2,1,0:T(8,128)(2,1)}, u32[]{:S(2)}, u32[]{:S(2)}) async-start(bf16[4,1024,512]{2,1,0:T(8,128)(2,1)} %broadcast_in_dim.57), calls=%async_computation.3 | async-start | bytes 8388608 | tf_op jit(solution)/shard_map/all_to_all | solution.py:47
  226.2 18.8 %all-to-all-start.3 = ((bf16[4,256,512]{2,1,0:T(8,128)(2,1)}), bf16[4,256,512]{2,1,0:T(8,128)(2,1)}, u32[]{:S(2)}, u32[]{:S(2)}) async-start(bf16[4,256,512]{2,1,0:T(8,128)(2,1)} %broadcast_in_dim.59), calls=%async_computation.4 | async-start | bytes 2097152 | tf_op jit(solution)/shard_map/all_to_all | solution.py:47
  230.5 167.4 %reduce-scatter.5.cloned.1.call-start = ((), (), s32[]{:S(2)}) async-start(), calls=%async_computation.10 | async-start | bytes 4456448 | tf_op jit(solution)/shard_map/reduce_scatter | solution.py:175
  249.2 11.2 %collective-permute-start.15 = (bf16[256,512]{1,0:T(8,128)(2,1)S(1)}, bf16[256,512]{1,0:T(8,128)(2,1)S(1)}, u32[]{:S(2)}, u32[]{:S(2)}) collective-permute-start(bf16[256,512]{1,0:T(8,128)(2,1)S(1)} %get-tuple-element.25), channel_id=1, source_target_pairs={{64,0},{65,1},{66,2},{67,3},{68,4},{69,5},{70,6},{71,7},{72,8},{73... | collective-permute-start | bytes 786440 | tf_op jit(solution)/shard_map/ppermute | solution.py:87
  265.4 18.7 %all-to-all-start.4 = ((bf16[4,256,512]{2,1,0:T(8,128)(2,1)}), bf16[4,256,512]{2,1,0:T(8,128)(2,1)}, u32[]{:S(2)}, u32[]{:S(2)}) async-start(bf16[4,256,512]{2,1,0:T(8,128)(2,1)} %broadcast_in_dim.60), calls=%async_computation.5 | async-start | bytes 2097152 | tf_op jit(solution)/shard_map/all_to_all | solution.py:47
  287.4 11.6 %collective-permute-start.16 = (bf16[256,512]{1,0:T(8,128)(2,1)S(1)}, bf16[256,512]{1,0:T(8,128)(2,1)}, u32[]{:S(2)}, u32[]{:S(2)}) collective-permute-start(bf16[256,512]{1,0:T(8,128)(2,1)S(1)} %get-tuple-element.23), channel_id=1, source_target_pairs={{64,0},{65,1},{66,2},{67,3},{68,4},{69,5},{70,6},{71,7},{72,8},{73... | collective-permute-start | bytes 786440 | tf_op jit(solution)/shard_map/ppermute | solution.py:87
  303.5 18.8 %all-to-all-start.5 = ((bf16[4,256,512]{2,1,0:T(8,128)(2,1)}), bf16[4,256,512]{2,1,0:T(8,128)(2,1)}, u32[]{:S(2)}, u32[]{:S(2)}) async-start(bf16[4,256,512]{2,1,0:T(8,128)(2,1)} %broadcast_in_dim.61), calls=%async_computation.6 | async-start | bytes 2097152 | tf_op jit(solution)/shard_map/all_to_all | solution.py:47
  325.6 11.2 %collective-permute-start.17 = (bf16[256,512]{1,0:T(8,128)(2,1)S(1)}, bf16[256,512]{1,0:T(8,128)(2,1)S(1)}, u32[]{:S(2)}, u32[]{:S(2)}) collective-permute-start(bf16[256,512]{1,0:T(8,128)(2,1)S(1)} %get-tuple-element.21), channel_id=1, source_target_pairs={{64,0},{65,1},{66,2},{67,3},{68,4},{69,5},{70,6},{71,7},{72,8},{73... | collective-permute-start | bytes 786440 | tf_op jit(solution)/shard_map/ppermute | solution.py:87
  340.0 18.7 %all-to-all-start.6 = ((bf16[4,256,512]{2,1,0:T(8,128)(2,1)}), bf16[4,256,512]{2,1,0:T(8,128)(2,1)}, u32[]{:S(2)}, u32[]{:S(2)}) async-start(bf16[4,256,512]{2,1,0:T(8,128)(2,1)} %broadcast_in_dim.62), calls=%async_computation.7 | async-start | bytes 2097152 | tf_op jit(solution)/shard_map/all_to_all | solution.py:47
  344.3 101.9 %reduce-scatter.7.cloned.1.call-start = ((), (), s32[]{:S(2)}) async-start(), calls=%async_computation.12 | async-start | bytes 1114112
  362.1 11.1 %collective-permute-start.18 = (bf16[256,512]{1,0:T(8,128)(2,1)S(1)}, bf16[256,512]{1,0:T(8,128)(2,1)S(1)}, u32[]{:S(2)}, u32[]{:S(2)}) collective-permute-start(bf16[256,512]{1,0:T(8,128)(2,1)S(1)} %get-tuple-element.19), channel_id=1, source_target_pairs={{64,0},{65,1},{66,2},{67,3},{68,4},{69,5},{70,6},{71,7},{72,8},{73... | collective-permute-start | bytes 786440 | tf_op jit(solution)/shard_map/ppermute | solution.py:87
  378.0 17.9 %all-to-all-start.7 = ((bf16[4,256,512]{2,1,0:T(8,128)(2,1)}), bf16[4,256,512]{2,1,0:T(8,128)(2,1)S(1)}, u32[]{:S(2)}, u32[]{:S(2)}) async-start(bf16[4,256,512]{2,1,0:T(8,128)(2,1)} %broadcast_in_dim.63), calls=%async_computation.8 | async-start | bytes 2097152 | tf_op jit(solution)/shard_map/all_to_all | solution.py:47
  381.6 67.2 %all-gather.2.cloned.1.call-start = ((), (), s32[]{:S(2)}) async-start(), calls=%async_computation.11 | async-start | bytes 3145728 | tf_op jit(solution)/shard_map/all_gather | solution.py:91
  (34 other events, 432.9 us)
Sparse Core Ops, SparseCore 0:
  260.6 77.3 reduce-scatter.4
  376.7 69.3 reduce-scatter.6
Sparse Core Ops, SparseCore 1:
  398.0 32.0 all-gather.1
